TPU v7x, 32 devices: a whole 2x2x4 slice. The times are simulated.
32 devices in a mesh: tile: 8 (over z, x), cls: 4 (over y, core).
Axes of the slice: x: 2, y: 2, z: 4, core: 2. Of those that a mesh axis runs over, the one named last changes fastest.
Arguments:
- concentration: float32 [64, 4, 16384], P('cls', None, 'tile'), may hold values from 0.05 to 2
- velocity: float32 [2, 4, 16384], P(None, None, 'tile'), may hold values from -0.3 to 0.3
- land_mask: int32 [16384], P('tile'), may hold values 0 or 1
- settling: float32 [64], P('cls'), may hold values from 0.01 to 0.3
- breakage_rate: float32 [64], replicated, may hold values from 0.02 to 0.3
- kernel_levels: int32 [64, 64], replicated, may hold values from 100 to 1000, as said below
- pair_target: int32 [64, 64], replicated, may hold values from 0 to 63, as said below
- fragment_weights: int32 [64, 64], replicated, may hold values from 1 to 16
Outputs:
- flocs: float32 [64, 4, 16384], P('cls', None, 'tile')
Inputs may be any that keep to these rules, and one draw needn't show every extreme that they name: `kernel_levels`: symmetric. `pair_target`: symmetric, and entry [i, j] is at least the larger of i and j.
All inputs are finite; a program needn't handle non-finite values. No bound on the sum of `land_mask` on one device may be relied on, other than what follows from the above.
Results may differ from a plain program's by a relative error of at most 0.0001.
Values sent between devices are 32-bit elements; how exact they have to be, the bound alone decides.
A program may use at most 64 MiB of HBM per device.

v0:
```python
import jax
import jax.numpy as jnp
from jax import lax
from jax.sharding import PartitionSpec as P

CY = 512
CX = 4
kernel_scale = 1e-05
temp_floats = 2097152


def passed_along(x, axis, by):
    length = lax.axis_size(axis)
    pairs = [(i, i + by) for i in range(length) if 0 <= i + by < length]
    return lax.ppermute(x, axis, pairs)


def face_flux(low, high, group, part):
    speed = 0.5 * (low[group + part] + high[group + part]) * low[group + 2] * high[group + 2]
    return jnp.maximum(speed, 0.0) * low[:group] + jnp.minimum(speed, 0.0) * high[:group]


def make_tables(start, count, kernel_levels, pair_target, fragment_weights, breakage_rate):
    total = kernel_levels.shape[0]
    levels = kernel_levels.astype(jnp.float32) * kernel_scale
    rank = jnp.arange(total, dtype=jnp.int32)
    mine = start + jnp.arange(count, dtype=jnp.int32)
    hit = pair_target[None, :, :] == mine[:, None, None]
    birth = jnp.where(hit, 0.5 * levels[None, :, :], 0.0)
    pairs = jnp.transpose(birth, (1, 0, 2)).reshape(total * count, total)
    lower = jnp.where(rank[:, None] <= rank[None, :], fragment_weights.astype(jnp.float32), 0.0)
    frag = lower / jnp.sum(lower, axis=0, keepdims=True)
    kernel_rows = lax.dynamic_slice_in_dim(levels, start, count, 0)
    frag_rows = lax.dynamic_slice_in_dim(frag, start, count, 0)
    rate_rows = lax.dynamic_slice_in_dim(breakage_rate, start, count, 0)
    return (pairs, kernel_rows, frag_rows, rate_rows)


def react(own, whole, tables, breakage_rate):
    pairs, kernel_rows, frag_rows, rate_rows = tables
    count, width = own.shape
    total = whole.shape[0]
    block = max(1, min(width, temp_floats // (total * count)))
    while width % block != 0:
        block = block - 1
    steps_count = width // block

    def add_block(index, gain):
        offset = index * block
        cols = lax.dynamic_slice_in_dim(whole, offset, block, 1)
        made = jnp.dot(
            pairs, cols, precision=lax.Precision.HIGHEST, preferred_element_type=jnp.float32
        )
        part_gain = jnp.sum(made.reshape(total, count, block) * cols[:, None, :], axis=0)
        return lax.dynamic_update_slice_in_dim(gain, part_gain, offset, 1)

    gain = lax.fori_loop(0, steps_count, add_block, jnp.zeros((count, width), jnp.float32))
    loss = own * jnp.dot(
        kernel_rows, whole, precision=lax.Precision.HIGHEST, preferred_element_type=jnp.float32
    )
    broken = (
        jnp.dot(
            frag_rows,
            breakage_rate[:, None] * whole,
            precision=lax.Precision.HIGHEST,
            preferred_element_type=jnp.float32,
        )
        - rate_rows[:, None] * own
    )
    return own + gain - loss + broken


def body(
    concentration,
    velocity,
    land_mask,
    settling,
    breakage_rate,
    kernel_levels,
    pair_target,
    fragment_weights,
):
    group, layers, columns = concentration.shape
    field = concentration.reshape(group, layers, CX, CY)
    water = land_mask.astype(jnp.float32).reshape(1, 1, CX, CY)
    stacked = jnp.concatenate(
        [field, velocity.reshape(2, layers, CX, CY), jnp.broadcast_to(water, (1, layers, CX, CY))],
        0,
    )
    west = passed_along(stacked[:, :, CX - 1 :, :], "tile", 1)
    east = passed_along(stacked[:, :, :1, :], "tile", -1)
    along_x = jnp.concatenate([west, stacked, east], 2)
    along_y = jnp.pad(stacked, ((0, 0), (0, 0), (0, 0), (1, 1)))
    flux_x = face_flux(along_x[:, :, :-1], along_x[:, :, 1:], group, 0)
    flux_y = face_flux(along_y[:, :, :, :-1], along_y[:, :, :, 1:], group, 1)
    moved = (
        field
        - (flux_x[:, :, 1:] - flux_x[:, :, :-1])
        - (flux_y[:, :, :, 1:] - flux_y[:, :, :, :-1])
    )
    sink = settling[:, None, None, None] * field
    moved = moved - sink + jnp.pad(sink[:, :-1], ((0, 0), (1, 0), (0, 0), (0, 0)))
    current = moved.reshape(group, layers * columns)
    start = lax.axis_index("cls") * group
    tables = make_tables(start, group, kernel_levels, pair_target, fragment_weights, breakage_rate)
    for sub in range(2):
        whole = lax.all_gather(current, "cls", axis=0, tiled=True)
        current = react(current, whole, tables, breakage_rate)
    return current.reshape(group, layers, columns)


def solution(mesh):
    return jax.shard_map(
        body,
        mesh=mesh,
        in_specs=(
            P("cls", None, "tile"),
            P(None, None, "tile"),
            P("tile"),
            P("cls"),
            P(),
            P(),
            P(),
            P(),
        ),
        out_specs=P("cls", None, "tile"),
        check_vma=False,
    )
```

profile of v0, /device:TPU:0, one launch (start us, length us, event | category | flops | bytes accessed | tf_op | source)
XLA Modules:
  0.0 164.2 jit_solution(15692153921223102179)
XLA Ops:
  6.5 1.5 reshape.47
  10.1 4.9 %collective-permute-start = (f32[19,4,1,512]{3,2,1,0:T(1,128)S(1)}, f32[19,4,1,512]{3,2,1,0:T(1,128)S(1)}, u32[]{:S(2)}, u32[]{:S(2)}) collective-permute-start(f32[19,4,1,512]{3,2,1,0:T(1,128)S(1)} %get-tuple-element.227), channel_id=1, source_target_pairs={{0,4},{4,8},{8,12},{12,16},{16,20},{20,24},{24,28},{1,5},{5,9},{9,... | collective-permute-start | bytes 466952 | tf_op jit(solution)/shard_map/ppermute | solution.py:15
  15.0 1.3 collective-permute-start.1
  17.1 1.2 collective-permute-done
  18.3 4.1 %collective-permute-done.1 = f32[19,4,1,512]{3,2,1,0:T(1,128)S(1)} collective-permute-done((f32[19,4,1,512]{3,2,1,0:T(1,128)S(1)}, f32[19,4,1,512]{3,2,1,0:T(1,128)S(1)}, u32[]{:S(2)}, u32[]{:S(2)}) %collective-permute-start.1) | collective-permute-done | bytes 155680 | tf_op jit(solution)/shard_map/ppermute | solution.py:15
  23.6 1.2 reshape.49
  25.2 23.7 %all-gather.3.cloned.1.call-done = f32[64,8192]{1,0:T(8,128)} async-done(((f32[16,8192]{1,0:T(8,128)}), f32[64,8192]{1,0:T(8,128)}) %all-gather.3.cloned.1.call-update) | async-done | bytes 2097168 | tf_op jit(solution)/shard_map/all_gather | solution.py:107
  49.0 37.6 %while.28 = (s32[]{:T(128)}, f32[16,8192]{1,0:T(8,128)S(1)}, f32[64,8192]{1,0:T(8,128)}, s32[64,64]{1,0:T(8,128)S(1)}, s32[1024]{0:T(1024)S(1)}, /*index=5*/f32[...) while((s32[]{:T(128)}, f32[16,8192]{1,0:T(8,128)S(1)}, f32[64,8192]{1,0:T(8,128)}, ...), condition=%wide.region_2.3_spmd.clone, body=%wide.region_0.2_spmd.clone.sunk | while | flops 1614905344 | bytes 19828892 | solution.py:57
  49.0 1.1 constant_dynamic-slice_fusion.4
  50.3 6.7 %fusion.53 = f32[2048,1024]{0,1:T(8,128)S(1)} fusion(f32[64,2048]{1,0:T(8,128)S(1)} %constant_dynamic-slice_fusion.4, f32[1024,64]{1,0:T(8,128)S(1)} %bitcast_select_fusion.4), kind=kOutput, calls=%fused_computation.77.clone.1 | convolution fusion | flops 1610612736 | bytes 9175040 | tf_op jit(solution)/shard_map/while/body/eval_jaxpr/dot_general | solution.py:51
  57.0 1.4 multiply_reduce_fusion.4
  59.7 6.7 %fusion.53 = f32[2048,1024]{0,1:T(8,128)S(1)} fusion(f32[64,2048]{1,0:T(8,128)S(1)} %constant_dynamic-slice_fusion.4, f32[1024,64]{1,0:T(8,128)S(1)} %bitcast_select_fusion.4), kind=kOutput, calls=%fused_computation.77.clone.1 | convolution fusion | flops 1610612736 | bytes 9175040 | tf_op jit(solution)/shard_map/while/body/eval_jaxpr/dot_general | solution.py:51
  66.4 1.4 multiply_reduce_fusion.4
  69.1 6.7 %fusion.53 = f32[2048,1024]{0,1:T(8,128)S(1)} fusion(f32[64,2048]{1,0:T(8,128)S(1)} %constant_dynamic-slice_fusion.4, f32[1024,64]{1,0:T(8,128)S(1)} %bitcast_select_fusion.4), kind=kOutput, calls=%fused_computation.77.clone.1 | convolution fusion | flops 1610612736 | bytes 9175040 | tf_op jit(solution)/shard_map/while/body/eval_jaxpr/dot_general | solution.py:51
  75.8 1.4 multiply_reduce_fusion.4
  78.5 6.7 %fusion.53 = f32[2048,1024]{0,1:T(8,128)S(1)} fusion(f32[64,2048]{1,0:T(8,128)S(1)} %constant_dynamic-slice_fusion.4, f32[1024,64]{1,0:T(8,128)S(1)} %bitcast_select_fusion.4), kind=kOutput, calls=%fused_computation.77.clone.1 | convolution fusion | flops 1610612736 | bytes 9175040 | tf_op jit(solution)/shard_map/while/body/eval_jaxpr/dot_general | solution.py:51
  85.2 1.4 multiply_reduce_fusion.4
  86.6 2.8 %fusion.7 = f32[16,8192]{1,0:T(8,128)S(1)} fusion(f32[16,8192]{1,0:T(8,128)S(1)} %copy-done.3, f32[64,8192]{1,0:T(8,128)} %get-tuple-element.368, f32[16,8192]{1,0:T(8,128)S(1)} %get-tuple-element.163, f32[64,64]{1,0:T(8,128)S(1)} %convert_element_type.14, s32[]{:T(128)S(6)} %select_n.32), kind=kOutput, calls=%fused_computation.19 | convolution fusion | flops 101057536 | bytes 3678212 | tf_op jit(solution)/shard_map/dot_general | solution.py:58
  89.5 2.0 %fusion.6 = f32[16,8192]{1,0:T(8,128)} fusion(f32[16,8192]{1,0:T(8,128)S(1)} %fusion.7, f32[64,8192]{1,0:T(8,128)S(1)} %copy-done, f32[64]{0:T(128)S(1)} %copy-done.7, f32[16,8192]{1,0:T(8,128)S(1)} %copy-done.3, f32[16]{0:T(128)S(1)} %dynamic_slice.25, f32[64,64]{1,0:T(8,128)S(1)} %get-tuple-element.230, s32[]{:T(128)S(6)} %select_n.32, ...), kind=kOutput, calls=%fused_computation.17 | convolution fusion | flops 101581824 | bytes 3679748 | tf_op jit(solution)/shard_map/dot_general | solution.py:62
  91.5 22.7 %all-gather.5.cloned.1.call-done = f32[64,8192]{1,0:T(8,128)} async-done(((f32[16,8192]{1,0:T(8,128)}), f32[64,8192]{1,0:T(8,128)}) %all-gather.5.cloned.1.call-update) | async-done | bytes 2097168 | tf_op jit(solution)/shard_map/all_gather | solution.py:107
  114.3 37.8 %while.29 = (s32[]{:T(128)}, f32[16,8192]{1,0:T(8,128)S(1)}, f32[64,8192]{1,0:T(8,128)}, s32[64,64]{1,0:T(8,128)S(1)}, s32[1024]{0:T(1024)S(1)}, /*index=5*/f32[...) while((s32[]{:T(128)}, f32[16,8192]{1,0:T(8,128)S(1)}, f32[64,8192]{1,0:T(8,128)}, ...), condition=%wide.region_6.7_spmd.clone, body=%wide.region_4.6_spmd.clone.sunk | while | flops 1614905344 | bytes 19828892 | solution.py:57
  115.8 6.7 %fusion.56 = f32[2048,1024]{0,1:T(8,128)S(1)} fusion(f32[64,2048]{1,0:T(8,128)S(1)} %constant_dynamic-slice_fusion.5, f32[1024,64]{1,0:T(8,128)S(1)} %bitcast_select_fusion.5), kind=kOutput, calls=%fused_computation.78.clone.1 | convolution fusion | flops 1610612736 | bytes 9175040 | tf_op jit(solution)/shard_map/while/body/eval_jaxpr/dot_general | solution.py:51
  122.5 1.4 multiply_reduce_fusion.5
  125.2 6.7 %fusion.56 = f32[2048,1024]{0,1:T(8,128)S(1)} fusion(f32[64,2048]{1,0:T(8,128)S(1)} %constant_dynamic-slice_fusion.5, f32[1024,64]{1,0:T(8,128)S(1)} %bitcast_select_fusion.5), kind=kOutput, calls=%fused_computation.78.clone.1 | convolution fusion | flops 1610612736 | bytes 9175040 | tf_op jit(solution)/shard_map/while/body/eval_jaxpr/dot_general | solution.py:51
  131.9 1.4 multiply_reduce_fusion.5
  134.6 6.7 %fusion.56 = f32[2048,1024]{0,1:T(8,128)S(1)} fusion(f32[64,2048]{1,0:T(8,128)S(1)} %constant_dynamic-slice_fusion.5, f32[1024,64]{1,0:T(8,128)S(1)} %bitcast_select_fusion.5), kind=kOutput, calls=%fused_computation.78.clone.1 | convolution fusion | flops 1610612736 | bytes 9175040 | tf_op jit(solution)/shard_map/while/body/eval_jaxpr/dot_general | solution.py:51
  141.3 1.4 multiply_reduce_fusion.5
  144.0 6.7 %fusion.56 = f32[2048,1024]{0,1:T(8,128)S(1)} fusion(f32[64,2048]{1,0:T(8,128)S(1)} %constant_dynamic-slice_fusion.5, f32[1024,64]{1,0:T(8,128)S(1)} %bitcast_select_fusion.5), kind=kOutput, calls=%fused_computation.78.clone.1 | convolution fusion | flops 1610612736 | bytes 9175040 | tf_op jit(solution)/shard_map/while/body/eval_jaxpr/dot_general | solution.py:51
  150.7 1.4 multiply_reduce_fusion.5
  152.1 2.8 %fusion.5 = f32[16,8192]{1,0:T(8,128)S(1)} fusion(f32[16,8192]{1,0:T(8,128)S(1)} %copy-done.2, f32[64,8192]{1,0:T(8,128)} %get-tuple-element.370, f32[16,8192]{1,0:T(8,128)S(1)} %get-tuple-element.164, f32[64,64]{1,0:T(8,128)S(1)} %convert_element_type.14, s32[]{:T(128)S(6)} %select_n.32), kind=kOutput, calls=%fused_computation.15 | convolution fusion | flops 101057536 | bytes 3678212 | tf_op jit(solution)/shard_map/dot_general | solution.py:58
  155.0 1.2 fusion.4
  156.2 1.1 reshape.50
  (69 shorter events, 13.8 us)
Async XLA Ops:
  6.5 9.9 %copy-start.8 = (f32[16]{0:T(128)S(1)}, f32[16]{0:T(128)}, u32[]{:S(2)}) copy-start(f32[16]{0:T(128)} %param.15) | copy-start | bytes 196
  6.5 42.4 %all-gather.3.cloned.1.call-start = ((), (), s32[]{:S(2)}) async-start(), calls=%async_computation | async-start | bytes 2621440 | tf_op jit(solution)/shard_map/all_gather | solution.py:107
  10.1 8.1 %collective-permute-start = (f32[19,4,1,512]{3,2,1,0:T(1,128)S(1)}, f32[19,4,1,512]{3,2,1,0:T(1,128)S(1)}, u32[]{:S(2)}, u32[]{:S(2)}) collective-permute-start(f32[19,4,1,512]{3,2,1,0:T(1,128)S(1)} %get-tuple-element.227), channel_id=1, source_target_pairs={{0,4},{4,8},{8,12},{12,16},{16,20},{20,24},{24,28},{1,5},{5,9},{9,... | collective-permute-start | bytes 466952 | tf_op jit(solution)/shard_map/ppermute | solution.py:15
  15.0 7.4 %collective-permute-start.1 = (f32[19,4,1,512]{3,2,1,0:T(1,128)S(1)}, f32[19,4,1,512]{3,2,1,0:T(1,128)S(1)}, u32[]{:S(2)}, u32[]{:S(2)}) collective-permute-start(f32[19,4,1,512]{3,2,1,0:T(1,128)S(1)} %get-tuple-element.228), channel_id=1, source_target_pairs={{4,0},{8,4},{12,8},{16,12},{20,16},{24,20},{28,24},{5,1},{9,5},{13... | collective-permute-start | bytes 466952 | tf_op jit(solution)/shard_map/ppermute | solution.py:15
  22.9 2.2 %copy-start.5 = (s32[64,64]{1,0:T(8,128)S(1)}, s32[64,64]{1,0:T(8,128)}, u32[]{:S(2)}) copy-start(s32[64,64]{1,0:T(8,128)} %param.17) | copy-start | bytes 49156
  22.9 2.2 %copy-start.7 = (f32[64]{0:T(128)S(1)}, f32[64]{0:T(128)}, u32[]{:S(2)}) copy-start(f32[64]{0:T(128)} %param.16) | copy-start | bytes 772
  22.9 2.3 %copy-start.6 = (s32[64,64]{1,0:T(8,128)S(1)}, s32[64,64]{1,0:T(8,128)}, u32[]{:S(2)}) copy-start(s32[64,64]{1,0:T(8,128)} %param.19) | copy-start | bytes 49156
  22.9 26.0 %copy-start.4 = (s32[64,64]{1,0:T(8,128)S(1)}, s32[64,64]{1,0:T(8,128)}, u32[]{:S(2)}) copy-start(s32[64,64]{1,0:T(8,128)} %param.18) | copy-start | bytes 49156
  24.8 89.5 %all-gather.5.cloned.1.call-start = ((), (), s32[]{:S(2)}) async-start(), calls=%async_computation.1 | async-start | bytes 2621440 | tf_op jit(solution)/shard_map/all_gather | solution.py:107
  49.0 37.6 %copy-start.3 = (f32[16,8192]{1,0:T(8,128)S(1)}, f32[16,8192]{1,0:T(8,128)}, u32[]{:S(2)}) copy-start(f32[16,8192]{1,0:T(8,128)} %reshape.49) | copy-start | bytes 1572868
  86.6 2.9 %copy-start = (f32[64,8192]{1,0:T(8,128)S(1)}, f32[64,8192]{1,0:T(8,128)}, u32[]{:S(2)}) copy-start(f32[64,8192]{1,0:T(8,128)} %get-tuple-element.368) | copy-start | bytes 6291460
  114.3 37.8 %copy-start.2 = (f32[16,8192]{1,0:T(8,128)S(1)}, f32[16,8192]{1,0:T(8,128)}, u32[]{:S(2)}) copy-start(f32[16,8192]{1,0:T(8,128)} %fusion.6) | copy-start | bytes 1572868
  152.1 2.9 %copy-start.1 = (f32[64,8192]{1,0:T(8,128)S(1)}, f32[64,8192]{1,0:T(8,128)}, u32[]{:S(2)}) copy-start(f32[64,8192]{1,0:T(8,128)} %get-tuple-element.370) | copy-start | bytes 6291460
Sparse Core Ops, SparseCore 0:
  24.9 23.9 all-gather.2
  91.7 22.5 all-gather.4
where the time goes:
time: 165 us; the launch traced here: 164 us
  matrix products  62.4 us (38%)
  waiting for transfers between devices  51.7 us (31%)
  other arithmetic  15.3 us (9%)
  local copies, waits for them, and re-layouts  14.1 us (9%)
  between operations  13.7 us (8%)
  starting transfers between devices  6.4 us (4%)
    dot_general x8, matrix products, add_block(): jnp.dot(pairs, cols, precision=lax.Precision.HIGHEST, preferred_element_t...  53.4 us
    all_gather x2, waiting for transfers between devices, body(): whole = lax.all_gather(current, 'cls', axis=0, tiled=True)  46.4 us
    reduce_sum x8, other arithmetic, add_block(): jnp.sum(made.reshape(total, count, block) * cols[:, None, :], axis=0)  10.9 us
    dynamic_slice x8, local copies, waits for them, and re-layouts, add_block(): cols = lax.dynamic_slice_in_dim(whole, offset, block, 1)  8.71 us
    ppermute x2, starting transfers between devices, passed_along(): return lax.ppermute(x, axis, pairs)  6.17 us
    dot_general x2, matrix products, react(): jnp.dot(kernel_rows, whole, precision=lax.Precision.HIGHEST, preferred_el...  5.69 us
    ppermute x2, waiting for transfers between devices, passed_along(): return lax.ppermute(x, axis, pairs)  5.32 us
  transfers between devices with their start and end apart: 4, of which 4 were waited for; matrix products, arithmetic and copies ran while one was open for 1% of the time, Pallas kernels for 0%

commit v1 on v0

--- a/solution.py
+++ b/solution.py
@@ -104,7 +104,14 @@
     start = lax.axis_index("cls") * group
     tables = make_tables(start, group, kernel_levels, pair_target, fragment_weights, breakage_rate)
     for sub in range(2):
-        whole = lax.all_gather(current, "cls", axis=0, tiled=True)
+        ring = [current]
+        for hop in range(3):
+            ring.append(lax.ppermute(ring[-1], "cls", [(dev, (dev + 1) % 4) for dev in range(4)]))
+        whole = jnp.roll(
+            jnp.concatenate(ring[::-1], axis=0),
+            (lax.axis_index("cls") + 1) * ring[0].shape[0],
+            axis=0,
+        )
         current = react(current, whole, tables, breakage_rate)
     return current.reshape(group, layers, columns)
 

time: 165 us -> 148 us (0.90)
  between operations: 13.7 us -> 0.26 us
  local copies, waits for them, and re-layouts: 14.1 us -> 6.25 us
  other arithmetic: 15.3 us -> 20.8 us
  matrix products: 62.4 us -> 58.1 us
  waiting for transfers between devices: 51.7 us -> 55.5 us
    ppermute x0 -> x6, waiting for transfers between devices: none -> 50.2 us  [body(): lax.ppermute(ring[-1], 'cls', [(dev, (dev + 1) % 4) for dev in range(4)])]
    all_gather x2 -> x0, waiting for transfers between devices: 46.4 us -> none  [body(): whole = lax.all_gather(current, 'cls', axis=0, tiled=True)]
    dynamic_slice x8, local copies, waits for them, and re-layouts: 8.71 us -> 0.34 us  [add_block(): cols = lax.dynamic_slice_in_dim(whole, offset, block, 1)]
    concatenate x0 -> x2, other arithmetic: none -> 5.51 us  [body(): jnp.roll(jnp.concatenate(ring[::-1], axis=0), (lax.axis_index('cls') + 1)...]
    dot_general x2, matrix products: 5.69 us -> 2.21 us  [react(): jnp.dot(kernel_rows, whole, precision=lax.Precision.HIGHEST, preferred_el...]
  transfers between devices with their start and end apart: 4 -> 8, of which waited for: 4 -> 8; matrix products, arithmetic and copies ran while one was open for 1% -> 1% of each run, Pallas kernels for 0% -> 0%
where the time goes in v1:
time: 148 us
  matrix products  58.1 us (39%)
  waiting for transfers between devices  55.5 us (38%)
  other arithmetic  20.8 us (14%)
  starting transfers between devices  6.3 us (4%)
  local copies, waits for them, and re-layouts  6.25 us (4%)
    dot_general x8, matrix products, add_block(): jnp.dot(pairs, cols, precision=lax.Precision.HIGHEST, preferred_element_t...  53.4 us
    ppermute x6, waiting for transfers between devices, body(): lax.ppermute(ring[-1], 'cls', [(dev, (dev + 1) % 4) for dev in range(4)])  50.2 us
    reduce_sum x8, other arithmetic, add_block(): jnp.sum(made.reshape(total, count, block) * cols[:, None, :], axis=0)  10.9 us
    ppermute x2, starting transfers between devices, passed_along(): return lax.ppermute(x, axis, pairs)  6.17 us
    concatenate x2, other arithmetic, body(): jnp.roll(jnp.concatenate(ring[::-1], axis=0), (lax.axis_index('cls') + 1)...  5.51 us
    ppermute x2, waiting for transfers between devices, passed_along(): return lax.ppermute(x, axis, pairs)  5.32 us
  transfers between devices with their start and end apart: 8, of which 8 were waited for; matrix products, arithmetic and copies ran while one was open for 1% of the time, Pallas kernels for 0%

profile of v1, /device:TPU:0, one launch (start us, length us, event | category | flops | bytes accessed | tf_op | source)
XLA Modules:
  0.0 148.0 jit_solution(4927708181805444738)
XLA Ops:
  0.0 1.5 %reshape.47 = f32[16,4,4,512]{3,2,1,0:T(4,128)S(1)} reshape(f32[16,4,2048]{2,1,0:T(4,128)} %param.14) | data formatting | bytes 1048576 | tf_op jit(solution)/shard_map/reshape | solution.py:84
  3.5 4.9 %collective-permute-start = (f32[19,4,1,512]{3,2,1,0:T(1,128)S(1)}, f32[19,4,1,512]{3,2,1,0:T(1,128)S(1)}, u32[]{:S(2)}, u32[]{:S(2)}) collective-permute-start(f32[19,4,1,512]{3,2,1,0:T(1,128)S(1)} %get-tuple-element.228), channel_id=1, source_target_pairs={{0,4},{4,8},{8,12},{12,16},{16,20},{20,24},{24,28},{1,5},{5,9},{9,... | collective-permute-start | bytes 466952 | tf_op jit(solution)/shard_map/ppermute | solution.py:15
  8.4 1.3 collective-permute-start.1
  11.7 4.1 %collective-permute-done.1 = f32[19,4,1,512]{3,2,1,0:T(1,128)S(1)} collective-permute-done((f32[19,4,1,512]{3,2,1,0:T(1,128)S(1)}, f32[19,4,1,512]{3,2,1,0:T(1,128)S(1)}, u32[]{:S(2)}, u32[]{:S(2)}) %collective-permute-start.1) | collective-permute-done | bytes 155680 | tf_op jit(solution)/shard_map/ppermute | solution.py:15
  17.4 8.6 %collective-permute-done.2 = f32[16,8192]{1,0:T(8,128)S(1)} collective-permute-done((f32[16,8192]{1,0:T(8,128)S(1)}, f32[16,8192]{1,0:T(8,128)S(1)}, u32[]{:S(2)}, u32[]{:S(2)}) %collective-permute-start.2) | collective-permute-done | bytes 524320 | tf_op jit(solution)/shard_map/ppermute | solution.py:109
  26.0 8.6 %collective-permute-done.3 = f32[16,8192]{1,0:T(8,128)S(1)} collective-permute-done((f32[16,8192]{1,0:T(8,128)S(1)}, f32[16,8192]{1,0:T(8,128)S(1)}, u32[]{:S(2)}, u32[]{:S(2)}) %collective-permute-start.3) | collective-permute-done | bytes 524320 | tf_op jit(solution)/shard_map/ppermute | solution.py:109
  35.4 7.9 %collective-permute-done.4 = f32[16,8192]{1,0:T(8,128)} collective-permute-done((f32[16,8192]{1,0:T(8,128)S(1)}, f32[16,8192]{1,0:T(8,128)}, u32[]{:S(2)}, u32[]{:S(2)}) %collective-permute-start.4) | collective-permute-done | bytes 524320 | tf_op jit(solution)/shard_map/ppermute | solution.py:109
  43.4 2.8 %fusion.18 = f32[64,8192]{1,0:T(8,128)S(1)} fusion(s32[]{:T(128)S(6)} %select_n.57, f32[16,8192]{1,0:T(8,128)} %collective-permute-done.4, f32[16,8192]{1,0:T(8,128)} %copy-done.1, f32[16,8192]{1,0:T(8,128)S(1)} %collective-permute-done.2, f32[16,8192]{1,0:T(8,128)S(1)} %reshape.49), kind=kLoop, calls=%fused_computation.46 | loop fusion | flops 3670016 | bytes 4194308 | tf_op jit(solution)/shard_map/jit(_roll_dynamic)/concatenate | solution.py:110
  46.2 33.6 %while.28 = (s32[]{:T(128)}, f32[16,8192]{1,0:T(8,128)S(1)}, f32[64,8192]{1,0:T(8,128)S(1)}, s32[64,64]{1,0:T(8,128)S(1)}, s32[1024]{0:T(1024)S(1)}, /*index=5*/...) while((s32[]{:T(128)}, f32[16,8192]{1,0:T(8,128)S(1)}, ...), condition=%wide.region_2.4_spmd.clone, body=%wide.region_0.3_spmd.clone.sunk | while | flops 1614905344 | bytes 19828892 | solution.py:57
  46.6 6.7 %fusion.65 = f32[2048,1024]{0,1:T(8,128)S(1)} fusion(f32[64,2048]{1,0:T(8,128)S(1)} %constant_dynamic-slice_fusion.4, f32[1024,64]{1,0:T(8,128)S(1)} %bitcast_select_fusion.4), kind=kOutput, calls=%fused_computation.105.clone.1 | convolution fusion | flops 1610612736 | bytes 9175040 | tf_op jit(solution)/shard_map/while/body/eval_jaxpr/dot_general | solution.py:51
  53.3 1.4 multiply_reduce_fusion.4
  55.0 6.7 %fusion.65 = f32[2048,1024]{0,1:T(8,128)S(1)} fusion(f32[64,2048]{1,0:T(8,128)S(1)} %constant_dynamic-slice_fusion.4, f32[1024,64]{1,0:T(8,128)S(1)} %bitcast_select_fusion.4), kind=kOutput, calls=%fused_computation.105.clone.1 | convolution fusion | flops 1610612736 | bytes 9175040 | tf_op jit(solution)/shard_map/while/body/eval_jaxpr/dot_general | solution.py:51
  61.7 1.4 multiply_reduce_fusion.4
  63.3 6.7 %fusion.65 = f32[2048,1024]{0,1:T(8,128)S(1)} fusion(f32[64,2048]{1,0:T(8,128)S(1)} %constant_dynamic-slice_fusion.4, f32[1024,64]{1,0:T(8,128)S(1)} %bitcast_select_fusion.4), kind=kOutput, calls=%fused_computation.105.clone.1 | convolution fusion | flops 1610612736 | bytes 9175040 | tf_op jit(solution)/shard_map/while/body/eval_jaxpr/dot_general | solution.py:51
  70.0 1.4 multiply_reduce_fusion.4
  71.7 6.7 %fusion.65 = f32[2048,1024]{0,1:T(8,128)S(1)} fusion(f32[64,2048]{1,0:T(8,128)S(1)} %constant_dynamic-slice_fusion.4, f32[1024,64]{1,0:T(8,128)S(1)} %bitcast_select_fusion.4), kind=kOutput, calls=%fused_computation.105.clone.1 | convolution fusion | flops 1610612736 | bytes 9175040 | tf_op jit(solution)/shard_map/while/body/eval_jaxpr/dot_general | solution.py:51
  78.4 1.4 multiply_reduce_fusion.4
  80.9 1.2 fusion.6
  82.2 8.6 %collective-permute-done.5 = f32[16,8192]{1,0:T(8,128)S(1)} collective-permute-done((f32[16,8192]{1,0:T(8,128)S(1)}, f32[16,8192]{1,0:T(8,128)S(1)}, u32[]{:S(2)}, u32[]{:S(2)}) %collective-permute-start.5) | collective-permute-done | bytes 524320 | tf_op jit(solution)/shard_map/ppermute | solution.py:109
  90.8 8.6 %collective-permute-done.6 = f32[16,8192]{1,0:T(8,128)S(1)} collective-permute-done((f32[16,8192]{1,0:T(8,128)S(1)}, f32[16,8192]{1,0:T(8,128)S(1)}, u32[]{:S(2)}, u32[]{:S(2)}) %collective-permute-start.6) | collective-permute-done | bytes 524320 | tf_op jit(solution)/shard_map/ppermute | solution.py:109
  100.2 7.9 %collective-permute-done.7 = f32[16,8192]{1,0:T(8,128)} collective-permute-done((f32[16,8192]{1,0:T(8,128)S(1)}, f32[16,8192]{1,0:T(8,128)}, u32[]{:S(2)}, u32[]{:S(2)}) %collective-permute-start.7) | collective-permute-done | bytes 524320 | tf_op jit(solution)/shard_map/ppermute | solution.py:109
  108.1 2.8 %fusion.11 = f32[64,8192]{1,0:T(8,128)S(1)} fusion(s32[]{:T(128)S(6)} %select_n.57, f32[16,8192]{1,0:T(8,128)} %collective-permute-done.7, f32[16,8192]{1,0:T(8,128)} %copy-done.2, f32[16,8192]{1,0:T(8,128)S(1)} %collective-permute-done.5, f32[16,8192]{1,0:T(8,128)S(1)} %fusion.6), kind=kLoop, calls=%fused_computation.39 | loop fusion | flops 3670016 | bytes 4194308 | tf_op jit(solution)/shard_map/jit(_roll_dynamic)/concatenate | solution.py:110
  110.9 33.6 %while.29 = (s32[]{:T(128)}, f32[16,8192]{1,0:T(8,128)S(1)}, f32[64,8192]{1,0:T(8,128)S(1)}, s32[64,64]{1,0:T(8,128)S(1)}, s32[1024]{0:T(1024)S(1)}, /*index=5*/...) while((s32[]{:T(128)}, f32[16,8192]{1,0:T(8,128)S(1)}, ...), condition=%wide.region_6.8_spmd.clone, body=%wide.region_4.7_spmd.clone.sunk | while | flops 1614905344 | bytes 19828892 | solution.py:57
  111.4 6.7 %fusion.68 = f32[2048,1024]{0,1:T(8,128)S(1)} fusion(f32[64,2048]{1,0:T(8,128)S(1)} %constant_dynamic-slice_fusion.5, f32[1024,64]{1,0:T(8,128)S(1)} %bitcast_select_fusion.5), kind=kOutput, calls=%fused_computation.106.clone.1 | convolution fusion | flops 1610612736 | bytes 9175040 | tf_op jit(solution)/shard_map/while/body/eval_jaxpr/dot_general | solution.py:51
  118.1 1.4 multiply_reduce_fusion.5
  119.8 6.7 %fusion.68 = f32[2048,1024]{0,1:T(8,128)S(1)} fusion(f32[64,2048]{1,0:T(8,128)S(1)} %constant_dynamic-slice_fusion.5, f32[1024,64]{1,0:T(8,128)S(1)} %bitcast_select_fusion.5), kind=kOutput, calls=%fused_computation.106.clone.1 | convolution fusion | flops 1610612736 | bytes 9175040 | tf_op jit(solution)/shard_map/while/body/eval_jaxpr/dot_general | solution.py:51
  126.4 1.4 multiply_reduce_fusion.5
  128.1 6.7 %fusion.68 = f32[2048,1024]{0,1:T(8,128)S(1)} fusion(f32[64,2048]{1,0:T(8,128)S(1)} %constant_dynamic-slice_fusion.5, f32[1024,64]{1,0:T(8,128)S(1)} %bitcast_select_fusion.5), kind=kOutput, calls=%fused_computation.106.clone.1 | convolution fusion | flops 1610612736 | bytes 9175040 | tf_op jit(solution)/shard_map/while/body/eval_jaxpr/dot_general | solution.py:51
  134.8 1.4 multiply_reduce_fusion.5
  136.5 6.7 %fusion.68 = f32[2048,1024]{0,1:T(8,128)S(1)} fusion(f32[64,2048]{1,0:T(8,128)S(1)} %constant_dynamic-slice_fusion.5, f32[1024,64]{1,0:T(8,128)S(1)} %bitcast_select_fusion.5), kind=kOutput, calls=%fused_computation.106.clone.1 | convolution fusion | flops 1610612736 | bytes 9175040 | tf_op jit(solution)/shard_map/while/body/eval_jaxpr/dot_general | solution.py:51
  143.1 1.4 multiply_reduce_fusion.5
  145.7 1.2 fusion.4
  (73 shorter events, 12.6 us)
Async XLA Ops:
  0.0 9.9 %copy-start.6 = (f32[16]{0:T(128)S(1)}, f32[16]{0:T(128)}, u32[]{:S(2)}) copy-start(f32[16]{0:T(128)} %param.17) | copy-start | bytes 196
  3.5 8.1 %collective-permute-start = (f32[19,4,1,512]{3,2,1,0:T(1,128)S(1)}, f32[19,4,1,512]{3,2,1,0:T(1,128)S(1)}, u32[]{:S(2)}, u32[]{:S(2)}) collective-permute-start(f32[19,4,1,512]{3,2,1,0:T(1,128)S(1)} %get-tuple-element.228), channel_id=1, source_target_pairs={{0,4},{4,8},{8,12},{12,16},{16,20},{20,24},{24,28},{1,5},{5,9},{9,... | collective-permute-start | bytes 466952 | tf_op jit(solution)/shard_map/ppermute | solution.py:15
  8.4 7.4 %collective-permute-start.1 = (f32[19,4,1,512]{3,2,1,0:T(1,128)S(1)}, f32[19,4,1,512]{3,2,1,0:T(1,128)S(1)}, u32[]{:S(2)}, u32[]{:S(2)}) collective-permute-start(f32[19,4,1,512]{3,2,1,0:T(1,128)S(1)} %get-tuple-element.229), channel_id=1, source_target_pairs={{4,0},{8,4},{12,8},{16,12},{20,16},{24,20},{28,24},{5,1},{9,5},{13... | collective-permute-start | bytes 466952 | tf_op jit(solution)/shard_map/ppermute | solution.py:15
  16.3 18.4 %copy-start.3 = (s32[64,64]{1,0:T(8,128)S(1)}, s32[64,64]{1,0:T(8,128)}, u32[]{:S(2)}) copy-start(s32[64,64]{1,0:T(8,128)} %param.19) | copy-start | bytes 49156
  16.3 18.4 %copy-start.5 = (f32[64]{0:T(128)S(1)}, f32[64]{0:T(128)}, u32[]{:S(2)}) copy-start(f32[64]{0:T(128)} %param.18) | copy-start | bytes 772
  16.4 18.5 %copy-start.4 = (s32[64,64]{1,0:T(8,128)S(1)}, s32[64,64]{1,0:T(8,128)}, u32[]{:S(2)}) copy-start(s32[64,64]{1,0:T(8,128)} %param.21) | copy-start | bytes 49156
  17.4 8.7 %collective-permute-start.2 = (f32[16,8192]{1,0:T(8,128)S(1)}, f32[16,8192]{1,0:T(8,128)S(1)}, u32[]{:S(2)}, u32[]{:S(2)}) collective-permute-start(f32[16,8192]{1,0:T(8,128)S(1)} %reshape.49), channel_id=1, source_target_pairs={{0,1},{1,2},{2,3},{3,0},{4,5},{5,6},{6,7},{7,4},{8,9},{9,10},{10,1... | collective-permute-start | bytes 1572872 | tf_op jit(solution)/shard_map/ppermute | solution.py:109
  26.0 8.6 %collective-permute-start.3 = (f32[16,8192]{1,0:T(8,128)S(1)}, f32[16,8192]{1,0:T(8,128)S(1)}, u32[]{:S(2)}, u32[]{:S(2)}) collective-permute-start(f32[16,8192]{1,0:T(8,128)S(1)} %collective-permute-done.2), channel_id=1, source_target_pairs={{0,1},{1,2},{2,3},{3,0},{4,5},{5,6},{6,7},{7,4},{8,9},{9,10},{10,1... | collective-permute-start | bytes 1572872 | tf_op jit(solution)/shard_map/ppermute | solution.py:109
  34.6 0.8 copy-start.1
  34.6 8.7 %collective-permute-start.4 = (f32[16,8192]{1,0:T(8,128)S(1)}, f32[16,8192]{1,0:T(8,128)}, u32[]{:S(2)}, u32[]{:S(2)}) collective-permute-start(f32[16,8192]{1,0:T(8,128)S(1)} %collective-permute-done.3), channel_id=1, source_target_pairs={{0,1},{1,2},{2,3},{3,0},{4,5},{5,6},{6,7},{7,4},{8,9},{9,10},{10,1... | collective-permute-start | bytes 1572872 | tf_op jit(solution)/shard_map/ppermute | solution.py:109
  35.4 10.7 %copy-start = (s32[64,64]{1,0:T(8,128)S(1)}, s32[64,64]{1,0:T(8,128)}, u32[]{:S(2)}) copy-start(s32[64,64]{1,0:T(8,128)} %param.20) | copy-start | bytes 49156
  82.1 8.7 %collective-permute-start.5 = (f32[16,8192]{1,0:T(8,128)S(1)}, f32[16,8192]{1,0:T(8,128)S(1)}, u32[]{:S(2)}, u32[]{:S(2)}) collective-permute-start(f32[16,8192]{1,0:T(8,128)S(1)} %fusion.6), channel_id=1, source_target_pairs={{0,1},{1,2},{2,3},{3,0},{4,5},{5,6},{6,7},{7,4},{8,9},{9,10},{10,1... | collective-permute-start | bytes 1572872 | tf_op jit(solution)/shard_map/ppermute | solution.py:109
  90.8 8.6 %collective-permute-start.6 = (f32[16,8192]{1,0:T(8,128)S(1)}, f32[16,8192]{1,0:T(8,128)S(1)}, u32[]{:S(2)}, u32[]{:S(2)}) collective-permute-start(f32[16,8192]{1,0:T(8,128)S(1)} %collective-permute-done.5), channel_id=1, source_target_pairs={{0,1},{1,2},{2,3},{3,0},{4,5},{5,6},{6,7},{7,4},{8,9},{9,10},{10,1... | collective-permute-start | bytes 1572872 | tf_op jit(solution)/shard_map/ppermute | solution.py:109
  99.4 0.8 copy-start.2
  99.4 8.7 %collective-permute-start.7 = (f32[16,8192]{1,0:T(8,128)S(1)}, f32[16,8192]{1,0:T(8,128)}, u32[]{:S(2)}, u32[]{:S(2)}) collective-permute-start(f32[16,8192]{1,0:T(8,128)S(1)} %collective-permute-done.6), channel_id=1, source_target_pairs={{0,1},{1,2},{2,3},{3,0},{4,5},{5,6},{6,7},{7,4},{8,9},{9,10},{10,1... | collective-permute-start | bytes 1572872 | tf_op jit(solution)/shard_map/ppermute | solution.py:109
